TPU v7x, 32 devices: a whole 2x2x4 slice. The times are simulated.
32 devices in a mesh: tok: 4 (over x, core), col: 8 (over z, y).
Axes of the slice: x: 2, y: 2, z: 4, core: 2. Of those that a mesh axis runs over, the one named last changes fastest.
Arguments:
- hidden_in: bfloat16 [1024, 36864], P('tok', 'col'), may hold values from -6 to 6
- down_weight: bfloat16 [4608, 36864], P('col', 'tok'), may hold values from -0.046875 to 0.046875
- keep_mask: int32 [4608, 36864], P('col', 'tok'), may hold values 0 or 1
Outputs:
- layer_out: bfloat16 [1024, 4608], P(('tok', 'col'))
- hessian: float32 [4608, 4608], P('col', 'tok')
All inputs are finite; a program needn't handle non-finite values. No bound on the sum of `keep_mask` on one device may be relied on, other than what follows from the above.
Results may differ from a plain program's by a relative error of at most 0.012.
Values may be sent and summed in bfloat16 or wider, within the bound.
No kernel may reach another device: no remote copies, remote signals or barrier semaphores. Data moves between devices by JAX's collectives and lax.ppermute only.
A program may use at most 192 MiB of HBM per device.

v0:
```python
import jax
import jax.numpy as jnp
from jax import lax
from jax.sharding import PartitionSpec as P


def contract_rows(left, right):
    return lax.dot_general(
        left, right, (((0,), (0,)), ((), ())), preferred_element_type=jnp.float32
    )


def contract_last(left, right):
    return lax.dot_general(
        left, right, (((1,), (1,)), ((), ())), preferred_element_type=jnp.float32
    )


def body(hidden_in, down_weight, keep_mask):
    pruned = down_weight * keep_mask.astype(down_weight.dtype)
    all_features = lax.all_gather(hidden_in, "col", axis=1, tiled=True)
    summed = contract_last(all_features, lax.all_gather(pruned, "tok", axis=1, tiled=True))
    layer_cols = summed.astype(jnp.bfloat16)
    scaling = 2.0 / (layer_cols.shape[0] * lax.axis_size("tok"))
    layer_out = lax.all_to_all(layer_cols, "col", split_axis=0, concat_axis=1, tiled=True)
    hessian_term = contract_rows(layer_cols, lax.all_gather(layer_cols, "col", axis=1, tiled=True))
    hessian = lax.psum_scatter(
        (hessian_term * scaling).astype(jnp.bfloat16), "tok", scatter_dimension=1, tiled=True
    ).astype(jnp.float32)
    return (layer_out, hessian)


def solution(mesh):
    in_specs = (P("tok", "col"), P("col", "tok"), P("col", "tok"))
    out_specs = (P(("tok", "col"), None), P("col", "tok"))
    return jax.shard_map(body, mesh=mesh, in_specs=in_specs, out_specs=out_specs, check_vma=False)
```

profile of v0, /device:TPU:0, one launch (start us, length us, event | category | flops | bytes accessed | tf_op | source)
XLA Modules:
  0.0 784.0 jit_solution(10702195190926574698)
XLA Ops:
  7.2 0.0 all-gather.6.cloned.1.call-start
  7.2 0.7 all-gather.6.cloned.1.call-update
  7.9 0.0 all-gather.4.cloned.1.call-start
  7.9 15.3 %convert_multiply_fusion = bf16[576,9216]{1,0:T(8,128)(2,1)} fusion(bf16[576,9216]{1,0:T(8,128)(2,1)} %param.4, s32[576,9216]{1,0:T(8,128)} %param.5), kind=kLoop, calls=%fused_computation.1 | loop fusion | flops 10616832 | bytes 42467328 | tf_op jit(solution)/shard_map/mul | solution.py:20
  23.2 0.0 all-gather.4.cloned.1.call-update
  23.3 0.0 all-gather.8.cloned.1.call-start
  23.3 351.4 %all-gather.6.cloned.1.call-done = bf16[256,36864]{1,0:T(8,128)(2,1)} async-done(((bf16[256,4608]{1,0:T(8,128)(2,1)}), bf16[256,36864]{1,0:T(8,128)(2,1)}) %all-gather.6.cloned.1.call-update) | async-done | bytes 18874384 | tf_op jit(solution)/shard_map/all_gather | solution.py:21
  374.7 254.7 %all-gather.4.cloned.1.call-done = bf16[576,36864]{1,0:T(8,128)(2,1)} async-done(((bf16[576,9216]{1,0:T(8,128)(2,1)}), bf16[576,36864]{1,0:T(8,128)(2,1)}) %all-gather.4.cloned.1.call-update) | async-done | bytes 42467344 | tf_op jit(solution)/shard_map/all_gather | solution.py:22
  629.4 23.3 %convolution_convert_fusion = bf16[576,256]{1,0:T(8,128)(2,1)} fusion(bf16[576,36864]{1,0:T(8,128)(2,1)} %all-gather.4.cloned.1.call-done, bf16[256,36864]{1,0:T(8,128)(2,1)} %all-gather.6.cloned.1.call-done), kind=kOutput, calls=%fused_computation.2 | convolution fusion | flops 10871783424 | bytes 61636608 | tf_op jit(solution)/shard_map/dot_general | solution.py:14
  652.7 0.0 all-gather.8.cloned.1.call-update
  652.8 0.0 reduce-scatter.4.cloned.1.call-start
  652.8 51.9 %all-gather.8.cloned.1.call-done = bf16[256,4608]{0,1:T(8,128)(2,1)} async-done(((bf16[256,576]{0,1:T(8,128)(2,1)}), bf16[256,4608]{0,1:T(8,128)(2,1)}) %all-gather.8.cloned.1.call-update) | async-done | bytes 2359312 | tf_op jit(solution)/shard_map/all_gather | solution.py:26
  704.7 5.8 multiply_convert_fusion
  710.5 0.0 copy-start
  710.5 8.4 %copy.11 = bf16[576,4608]{0,1:T(8,128)(2,1)} copy(bf16[576,4608]{1,0:T(8,128)(2,1)} %multiply_convert_fusion) | data formatting | bytes 10616832
  718.9 0.0 reduce-scatter.4.cloned.1.call-update
  719.0 0.0 copy-done
  719.0 0.2 copy.9
  719.2 13.3 %all_to_all.19 = bf16[8,32,576]{2,1,0:T(8,128)(2,1)S(1)} all-to-all(bf16[8,32,576]{2,1,0:T(8,128)(2,1)S(1)} %bitcast.13), channel_id=1, replica_groups=mesh['tok'=4,'col'=8] {'col'}, dimensions={0} | all-to-all | bytes 589824 | tf_op jit(solution)/shard_map/all_to_all | solution.py:25
  732.5 0.1 copy.10
  732.6 1.0 all_to_all.17
  733.6 40.3 %reduce-scatter.4.cloned.1.call-done = bf16[1152,576]{1,0:T(8,128)(2,1)} async-done(((bf16[4608,576]{1,0:T(8,128)(2,1)}), bf16[1152,576]{1,0:T(8,128)(2,1)}) %reduce-scatter.4.cloned.1.call-update) | async-done | bytes 1327120
  773.8 1.9 copy.12
  775.7 1.7 convert_element_type.19
Async XLA Ops:
  7.2 367.5 %all-gather.6.cloned.1.call-start = ((), (), s32[]{:S(2)}) async-start(), calls=%async_computation.3 | async-start | bytes 21233664 | tf_op jit(solution)/shard_map/all_gather | solution.py:21
  7.9 621.5 %all-gather.4.cloned.1.call-start = ((), (), s32[]{:S(2)}) async-start(), calls=%async_computation.2 | async-start | bytes 53084160 | tf_op jit(solution)/shard_map/all_gather | solution.py:22
  23.3 681.5 %all-gather.8.cloned.1.call-start = ((), (), s32[]{:S(2)}) async-start(), calls=%async_computation.4 | async-start | bytes 2654208 | tf_op jit(solution)/shard_map/all_gather | solution.py:26
  652.8 121.1 %reduce-scatter.4.cloned.1.call-start = ((), (), s32[]{:S(2)}) async-start(), calls=%async_computation.5 | async-start | bytes 7372800
  710.5 8.5 %copy-start = (bf16[576,256]{1,0:T(8,128)(2,1)S(1)}, bf16[576,256]{1,0:T(8,128)(2,1)}, u32[]{:S(2)}) copy-start(bf16[576,256]{1,0:T(8,128)(2,1)} %convolution_convert_fusion) | copy-start | bytes 884740
Sparse Core Ops, SparseCore 0:
  9.5 365.1 all-gather.5
  376.2 253.1 all-gather.3
  652.9 51.8 all-gather.7
  719.1 54.7 reduce-scatter.3
where the time goes:
time: 784 us
  waiting for transfers between devices  699 us (89%)
  matrix products  29.1 us (4%)
  other arithmetic  17 us (2%)
  between operations  13.8 us (2%)
  blocking collectives  13.3 us (2%)
  local copies, waits for them, and re-layouts  11.6 us (1%)
    all_gather x1, waiting for transfers between devices, body(): all_features = lax.all_gather(hidden_in, 'col', axis=1, tiled=True)  351 us
    all_gather x1, waiting for transfers between devices, body(): lax.all_gather(pruned, 'tok', axis=1, tiled=True)  255 us
    all_gather x1, waiting for transfers between devices, body(): lax.all_gather(layer_cols, 'col', axis=1, tiled=True)  51.9 us
    unnamed x5, waiting for transfers between devices  41 us
    dot_general x1, matrix products, contract_last(): lax.dot_general(left, right, (((1,), (1,)), ((), ())), preferred_element_...  23.3 us
  transfers between devices with their start and end apart: 4, of which 4 were waited for; matrix products, arithmetic and copies ran while one was open for 2% of the time, Pallas kernels for 0%

commit v1 on v0

--- a/solution.py
+++ b/solution.py
@@ -18,7 +18,22 @@
 
 def body(hidden_in, down_weight, keep_mask):
     pruned = down_weight * keep_mask.astype(down_weight.dtype)
-    all_features = lax.all_gather(hidden_in, "col", axis=1, tiled=True)
+
+    def take_points(inp, axis_tag, d_out):
+        n_parts = lax.psum(1, axis_name=axis_tag)
+        back = sorted(((dev_j, (dev_j + 1) % n_parts) for dev_j in range(n_parts)))
+        block_now = inp
+        shelf = [block_now]
+        for p in [*range(1, n_parts)]:
+            block_now = lax.ppermute(block_now, axis_name=axis_tag, perm=back)
+            shelf.insert(0, block_now)
+        return jnp.roll(
+            jnp.concatenate(shelf, axis=d_out),
+            shift=(lax.axis_index(axis_tag) + 1) * inp.shape[d_out],
+            axis=d_out,
+        )
+
+    all_features = take_points(hidden_in, "col", 1)
     summed = contract_last(all_features, lax.all_gather(pruned, "tok", axis=1, tiled=True))
     layer_cols = summed.astype(jnp.bfloat16)
     scaling = 2.0 / (layer_cols.shape[0] * lax.axis_size("tok"))

time: 784 us -> 597 us (0.76)
  waiting for transfers between devices: 699 us -> 460 us
  local copies, waits for them, and re-layouts: 11.6 us -> 60 us
    ppermute x0 -> x7, waiting for transfers between devices: none -> 372 us  [take_points(): block_now = lax.ppermute(block_now, axis_name=axis_tag, perm=back)]
    all_gather x1 -> x0, waiting for transfers between devices: 351 us -> none  [body(): all_features = lax.all_gather(hidden_in, 'col', axis=1, tiled=True)]
    all_gather x1, waiting for transfers between devices: 255 us -> 0.01 us  [body(): lax.all_gather(pruned, 'tok', axis=1, tiled=True)]
    unnamed x4 -> x39, local copies, waits for them, and re-layouts: 10.3 us -> 56.2 us
    unnamed x5 -> x4, waiting for transfers between devices: 41 us -> 39.4 us
  transfers between devices with their start and end apart: 4 -> 10, of which waited for: 4 -> 9; matrix products, arithmetic and copies ran while one was open for 2% -> 7% of each run, Pallas kernels for 0% -> 0%
where the time goes in v1:
time: 597 us; the launch traced here: 596 us
  waiting for transfers between devices  460 us (77%)
  local copies, waits for them, and re-layouts  60 us (10%)
  matrix products  29.2 us (5%)
  other arithmetic  16.4 us (3%)
  between operations  13.8 us (2%)
  blocking collectives  13.3 us (2%)
    ppermute x7, waiting for transfers between devices, take_points(): block_now = lax.ppermute(block_now, axis_name=axis_tag, perm=back)  372 us
    unnamed x39, local copies, waits for them, and re-layouts  56.2 us
    all_gather x1, waiting for transfers between devices, body(): lax.all_gather(layer_cols, 'col', axis=1, tiled=True)  48.2 us
    unnamed x4, waiting for transfers between devices  39.4 us
    dot_general x1, matrix products, contract_last(): lax.dot_general(left, right, (((1,), (1,)), ((), ())), preferred_element_...  23.4 us
    mul x1, other arithmetic, body(): pruned = down_weight * keep_mask.astype(down_weight.dtype)  14.7 us
    all_to_all x1, blocking collectives, body(): lax.all_to_all(layer_cols, 'col', split_axis=0, concat_axis=1, tiled=True)  13.3 us
  transfers between devices with their start and end apart: 10, of which 9 were waited for; matrix products, arithmetic and copies ran while one was open for 7% of the time, Pallas kernels for 0%

profile of v1, /device:TPU:0, one launch (start us, length us, event | category | flops | bytes accessed | tf_op | source)
XLA Modules:
  0.0 596.0 jit_solution(3892642806917026979)
XLA Ops:
  7.2 0.0 all-gather.3.cloned.1.call-start
  7.2 14.7 %convert_multiply_fusion = bf16[576,9216]{1,0:T(8,128)(2,1)} fusion(bf16[576,9216]{1,0:T(8,128)(2,1)} %param.4, s32[576,9216]{1,0:T(8,128)} %param.5), kind=kLoop, calls=%fused_computation.3 | loop fusion | flops 10616832 | bytes 42467328 | tf_op jit(solution)/shard_map/mul | solution.py:20
  22.0 0.0 all-gather.3.cloned.1.call-update
  22.0 0.0 all-gather.5.cloned.1.call-start
  22.0 3.0 collective-permute-start
  25.1 54.3 %collective-permute-done = bf16[256,4608]{1,0:T(8,128)(2,1)S(1)} collective-permute-done((bf16[256,4608]{1,0:T(8,128)(2,1)S(1)}, bf16[256,4608]{1,0:T(8,128)(2,1)S(1)}, u32[]{:S(2)}, u32[]{:S(2)}) %collective-permute-start) | collective-permute-done | bytes 2359328 | tf_op jit(solution)/shard_map/ppermute | solution.py:28
  79.4 1.5 copy-done.1
  80.8 0.0 collective-permute-start.1
  80.8 55.1 %collective-permute-done.1 = bf16[256,4608]{1,0:T(8,128)(2,1)S(1)} collective-permute-done((bf16[256,4608]{1,0:T(8,128)(2,1)S(1)}, bf16[256,4608]{1,0:T(8,128)(2,1)S(1)}, u32[]{:S(2)}, u32[]{:S(2)}) %collective-permute-start.1) | collective-permute-done | bytes 2359328 | tf_op jit(solution)/shard_map/ppermute | solution.py:28
  136.0 1.4 copy-done.3
  137.4 54.2 %collective-permute-done.2 = bf16[256,4608]{1,0:T(8,128)(2,1)S(1)} collective-permute-done((bf16[256,4608]{1,0:T(8,128)(2,1)S(1)}, bf16[256,4608]{1,0:T(8,128)(2,1)S(1)}, u32[]{:S(2)}, u32[]{:S(2)}) %collective-permute-start.2) | collective-permute-done | bytes 2359328 | tf_op jit(solution)/shard_map/ppermute | solution.py:28
  191.6 1.5 copy-done.5
  193.1 53.4 %collective-permute-done.3 = bf16[256,4608]{1,0:T(8,128)(2,1)S(1)} collective-permute-done((bf16[256,4608]{1,0:T(8,128)(2,1)S(1)}, bf16[256,4608]{1,0:T(8,128)(2,1)S(1)}, u32[]{:S(2)}, u32[]{:S(2)}) %collective-permute-start.3) | collective-permute-done | bytes 2359328 | tf_op jit(solution)/shard_map/ppermute | solution.py:28
  246.5 1.4 copy-done.7
  247.9 52.5 %collective-permute-done.4 = bf16[256,4608]{1,0:T(8,128)(2,1)S(1)} collective-permute-done((bf16[256,4608]{1,0:T(8,128)(2,1)S(1)}, bf16[256,4608]{1,0:T(8,128)(2,1)S(1)}, u32[]{:S(2)}, u32[]{:S(2)}) %collective-permute-start.4) | collective-permute-done | bytes 2359328 | tf_op jit(solution)/shard_map/ppermute | solution.py:28
  300.5 1.4 copy-done.9
  301.9 51.8 %collective-permute-done.5 = bf16[256,4608]{1,0:T(8,128)(2,1)} collective-permute-done((bf16[256,4608]{1,0:T(8,128)(2,1)S(1)}, bf16[256,4608]{1,0:T(8,128)(2,1)}, u32[]{:S(2)}, u32[]{:S(2)}) %collective-permute-start.5) | collective-permute-done | bytes 2359328 | tf_op jit(solution)/shard_map/ppermute | solution.py:28
  353.7 51.1 %collective-permute-done.6 = bf16[256,4608]{1,0:T(8,128)(2,1)} collective-permute-done((bf16[256,4608]{1,0:T(8,128)(2,1)}, bf16[256,4608]{1,0:T(8,128)(2,1)}, u32[]{:S(2)}, u32[]{:S(2)}) %collective-permute-start.6) | collective-permute-done | bytes 2359328 | tf_op jit(solution)/shard_map/ppermute | solution.py:28
  404.8 3.2 constant_dynamic-update-slice_fusion.15
  408.0 3.2 constant_dynamic-update-slice_fusion.14
  411.3 3.2 constant_dynamic-update-slice_fusion.13
  414.5 3.3 constant_dynamic-update-slice_fusion.12
  417.8 3.2 constant_dynamic-update-slice_fusion.11
  421.0 3.2 constant_dynamic-update-slice_fusion.10
  424.3 3.3 constant_dynamic-update-slice_fusion.9
  427.5 1.6 constant_dynamic-update-slice_fusion.8
  429.1 3.2 constant_dynamic-update-slice_fusion.7
  432.3 3.2 constant_dynamic-update-slice_fusion.6
  435.6 1.6 constant_dynamic-update-slice_fusion.5
  437.2 1.6 constant_dynamic-update-slice_fusion.4
  438.8 1.6 constant_dynamic-update-slice_fusion.3
  440.4 1.6 constant_dynamic-update-slice_fusion.2
  442.0 1.6 constant_dynamic-update-slice_fusion.1
  443.6 1.6 constant_dynamic-update-slice_fusion
  445.1 23.4 %fusion.2 = bf16[256,576]{0,1:T(8,128)(2,1)} fusion(bf16[576,36864]{1,0:T(8,128)(2,1)} %all-gather.3.cloned.1.call-done, bf16[256,73728]{1,0:T(8,128)(2,1)} %constant_dynamic-update-slice_fusion, s32[]{:T(128)S(6)} %select_n.14), kind=kOutput, calls=%fused_computation.4 | convolution fusion | flops 10871783424 | bytes 61636612 | tf_op jit(solution)/shard_map/dot_general | solution.py:14
  468.6 0.0 all-gather.5.cloned.1.call-update
  468.6 0.0 reduce-scatter.4.cloned.1.call-start
  468.6 48.2 %all-gather.5.cloned.1.call-done = bf16[256,4608]{0,1:T(8,128)(2,1)} async-done(((bf16[256,576]{0,1:T(8,128)(2,1)}), bf16[256,4608]{0,1:T(8,128)(2,1)}) %all-gather.5.cloned.1.call-update) | async-done | bytes 2359312 | tf_op jit(solution)/shard_map/all_gather | solution.py:41
  516.8 5.8 multiply_convert_fusion
  522.6 8.4 %copy.11 = bf16[576,4608]{0,1:T(8,128)(2,1)} copy(bf16[576,4608]{1,0:T(8,128)(2,1)} %multiply_convert_fusion) | data formatting | bytes 10616832
  531.0 0.0 reduce-scatter.4.cloned.1.call-update
  531.0 1.2 copy.9
  532.2 13.3 %all_to_all.19 = bf16[8,32,576]{2,1,0:T(8,128)(2,1)S(1)} all-to-all(bf16[8,32,576]{2,1,0:T(8,128)(2,1)S(1)} %bitcast.9), channel_id=1, replica_groups=mesh['tok'=4,'col'=8] {'col'}, dimensions={0} | all-to-all | bytes 589824 | tf_op jit(solution)/shard_map/all_to_all | solution.py:40
  545.5 0.1 copy.10
  545.6 1.0 all_to_all.17
  546.6 39.3 %reduce-scatter.4.cloned.1.call-done = bf16[1152,576]{1,0:T(8,128)(2,1)} async-done(((bf16[4608,576]{1,0:T(8,128)(2,1)}), bf16[1152,576]{1,0:T(8,128)(2,1)}) %reduce-scatter.4.cloned.1.call-update) | async-done | bytes 1327120
  585.9 1.9 copy.12
  587.8 1.7 convert_element_type.15
  (23 shorter events, 0.0 us)
Async XLA Ops:
  7.2 14.9 %copy-start = (bf16[256,4608]{1,0:T(8,128)(2,1)S(1)}, bf16[256,4608]{1,0:T(8,128)(2,1)}, u32[]{:S(2)}) copy-start(bf16[256,4608]{1,0:T(8,128)(2,1)} %param.3) | copy-start | bytes 7077892
  7.2 437.9 %all-gather.3.cloned.1.call-start = ((), (), s32[]{:S(2)}) async-start(), calls=%async_computation.2 | async-start | bytes 53084160 | tf_op jit(solution)/shard_map/all_gather | solution.py:37
  22.0 494.9 %all-gather.5.cloned.1.call-start = ((), (), s32[]{:S(2)}) async-start(), calls=%async_computation.3 | async-start | bytes 2654208 | tf_op jit(solution)/shard_map/all_gather | solution.py:41
  22.0 57.3 %collective-permute-start = (bf16[256,4608]{1,0:T(8,128)(2,1)S(1)}, bf16[256,4608]{1,0:T(8,128)(2,1)S(1)}, u32[]{:S(2)}, u32[]{:S(2)}) collective-permute-start(bf16[256,4608]{1,0:T(8,128)(2,1)S(1)} %copy-done), channel_id=1, source_target_pairs={{0,1},{1,2},{2,3},{3,4},{4,5},{5,6},{6,7},{7,0},{8,9},{9,10},{10,1... | collective-permute-start | bytes 7077896 | tf_op jit(solution)/shard_map/ppermute | solution.py:28
  79.4 1.5 copy-start.1
  80.8 55.1 %collective-permute-start.1 = (bf16[256,4608]{1,0:T(8,128)(2,1)S(1)}, bf16[256,4608]{1,0:T(8,128)(2,1)S(1)}, u32[]{:S(2)}, u32[]{:S(2)}) collective-permute-start(bf16[256,4608]{1,0:T(8,128)(2,1)S(1)} %collective-permute-done), channel_id=1, source_target_pairs={{0,1},{1,2},{2,3},{3,4},{4,5},{5,6},{6,7},{7,0},{8,9},{9,10},{10,1... | collective-permute-start | bytes 7077896 | tf_op jit(solution)/shard_map/ppermute | solution.py:28
  136.0 1.4 copy-start.3
  137.4 54.3 %collective-permute-start.2 = (bf16[256,4608]{1,0:T(8,128)(2,1)S(1)}, bf16[256,4608]{1,0:T(8,128)(2,1)S(1)}, u32[]{:S(2)}, u32[]{:S(2)}) collective-permute-start(bf16[256,4608]{1,0:T(8,128)(2,1)S(1)} %collective-permute-done.1), channel_id=1, source_target_pairs={{0,1},{1,2},{2,3},{3,4},{4,5},{5,6},{6,7},{7,0},{8,9},{9,10},{10,1... | collective-permute-start | bytes 7077896 | tf_op jit(solution)/shard_map/ppermute | solution.py:28
  191.6 1.5 copy-start.5
  193.1 53.4 %collective-permute-start.3 = (bf16[256,4608]{1,0:T(8,128)(2,1)S(1)}, bf16[256,4608]{1,0:T(8,128)(2,1)S(1)}, u32[]{:S(2)}, u32[]{:S(2)}) collective-permute-start(bf16[256,4608]{1,0:T(8,128)(2,1)S(1)} %collective-permute-done.2), channel_id=1, source_target_pairs={{0,1},{1,2},{2,3},{3,4},{4,5},{5,6},{6,7},{7,0},{8,9},{9,10},{10,1... | collective-permute-start | bytes 7077896 | tf_op jit(solution)/shard_map/ppermute | solution.py:28
  246.5 1.4 copy-start.7
  247.9 52.5 %collective-permute-start.4 = (bf16[256,4608]{1,0:T(8,128)(2,1)S(1)}, bf16[256,4608]{1,0:T(8,128)(2,1)S(1)}, u32[]{:S(2)}, u32[]{:S(2)}) collective-permute-start(bf16[256,4608]{1,0:T(8,128)(2,1)S(1)} %collective-permute-done.3), channel_id=1, source_target_pairs={{0,1},{1,2},{2,3},{3,4},{4,5},{5,6},{6,7},{7,0},{8,9},{9,10},{10,1... | collective-permute-start | bytes 7077896 | tf_op jit(solution)/shard_map/ppermute | solution.py:28
  300.5 1.4 copy-start.9
  301.9 51.8 %collective-permute-start.5 = (bf16[256,4608]{1,0:T(8,128)(2,1)S(1)}, bf16[256,4608]{1,0:T(8,128)(2,1)}, u32[]{:S(2)}, u32[]{:S(2)}) collective-permute-start(bf16[256,4608]{1,0:T(8,128)(2,1)S(1)} %collective-permute-done.4), channel_id=1, source_target_pairs={{0,1},{1,2},{2,3},{3,4},{4,5},{5,6},{6,7},{7,0},{8,9},{9,10},{10,1... | collective-permute-start | bytes 7077896 | tf_op jit(solution)/shard_map/ppermute | solution.py:28
  353.7 51.1 %collective-permute-start.6 = (bf16[256,4608]{1,0:T(8,128)(2,1)}, bf16[256,4608]{1,0:T(8,128)(2,1)}, u32[]{:S(2)}, u32[]{:S(2)}) collective-permute-start(bf16[256,4608]{1,0:T(8,128)(2,1)} %collective-permute-done.5), channel_id=1, source_target_pairs={{0,1},{1,2},{2,3},{3,4},{4,5},{5,6},{6,7},{7,0},{8,9},{9,10},{10,1... | collective-permute-start | bytes 7077896 | tf_op jit(solution)/shard_map/ppermute | solution.py:28
  353.7 81.9 %copy-start.10 = (bf16[256,4608]{1,0:T(8,128)(2,1)S(1)}, bf16[256,4608]{1,0:T(8,128)(2,1)}, u32[]{:S(2)}) copy-start(bf16[256,4608]{1,0:T(8,128)(2,1)} %copy-done.9) | copy-start | bytes 7077892
  353.7 83.5 %copy-start.8 = (bf16[256,4608]{1,0:T(8,128)(2,1)S(1)}, bf16[256,4608]{1,0:T(8,128)(2,1)}, u32[]{:S(2)}) copy-start(bf16[256,4608]{1,0:T(8,128)(2,1)} %copy-done.7) | copy-start | bytes 7077892
  353.7 85.1 %copy-start.6 = (bf16[256,4608]{1,0:T(8,128)(2,1)S(1)}, bf16[256,4608]{1,0:T(8,128)(2,1)}, u32[]{:S(2)}) copy-start(bf16[256,4608]{1,0:T(8,128)(2,1)} %copy-done.5) | copy-start | bytes 7077892
  353.7 86.7 %copy-start.4 = (bf16[256,4608]{1,0:T(8,128)(2,1)S(1)}, bf16[256,4608]{1,0:T(8,128)(2,1)}, u32[]{:S(2)}) copy-start(bf16[256,4608]{1,0:T(8,128)(2,1)} %copy-done.3) | copy-start | bytes 7077892
  353.7 88.3 %copy-start.2 = (bf16[256,4608]{1,0:T(8,128)(2,1)S(1)}, bf16[256,4608]{1,0:T(8,128)(2,1)}, u32[]{:S(2)}) copy-start(bf16[256,4608]{1,0:T(8,128)(2,1)} %copy-done.1) | copy-start | bytes 7077892
  468.6 117.3 %reduce-scatter.4.cloned.1.call-start = ((), (), s32[]{:S(2)}) async-start(), calls=%async_computation.4 | async-start | bytes 7372800
Sparse Core Ops, SparseCore 0:
  22.1 255.8 all-gather.2
  468.7 48.0 all-gather.4
  531.1 54.7 reduce-scatter.3
